TPU v7x, 32 devices: a whole 2x2x4 slice. The times are simulated.
32 devices in a mesh: ep: 8 (over y, x, core), tp: 4 (over z).
Axes of the slice: x: 2, y: 2, z: 4, core: 2. Of those that a mesh axis runs over, the one named last changes fastest.
Arguments:
- tokens: bfloat16 [5120, 2048], P('ep'), may hold values from -6 to 6
- norm1_gain: float32 [2048], replicated, may hold values from 0.1 to 1.9
- w_qkv: bfloat16 [3, 2048, 2048], P(None, None, 'tp'), may hold values from -0.125 to 0.125
- b_qkv: bfloat16 [3, 16, 128], P(None, 'tp'), may hold values from -3 to 3
- w_out: bfloat16 [2048, 2048], P('tp'), may hold values from -1.25 to 1.25
- norm2_gain: float32 [2048], replicated, may hold values from 0.1 to 1.9
- w_router: bfloat16 [2048, 8], replicated, may hold values from -0.0625 to 0.0625
- w_sgate: bfloat16 [2048], replicated, may hold values from -0.125 to 0.125
- w_shared_gu: bfloat16 [2, 2048, 5632], P(None, None, 'tp'), may hold values from -0.125 to 0.125
- w_shared_down: bfloat16 [5632, 2048], P('tp'), may hold values from -0.15625 to 0.15625
- w_expert_gu: bfloat16 [8, 2, 2048, 1408], P('ep', None, None, 'tp'), may hold values from -0.125 to 0.125
- w_expert_down: bfloat16 [8, 1408, 2048], P('ep', 'tp'), may hold values from -0.3125 to 0.3125
- routes: int32 [5120, 4], P('ep'), may hold values from 0 to 7, all different within a row; in each aligned block of 640 rows (0 to 639, 640 to 1279, ...) at most 400 rows name the same one
- grad_out: bfloat16 [5120, 2048], P('ep'), may hold values from -6 to 6
Outputs:
- output: bfloat16 [5120, 2048], P(('ep', 'tp'))
- grad_tokens: float32 [5120, 2048], P(('ep', 'tp'))
- grad_norm1_gain: float32 [2048], P('ep')
- grad_w_qkv: float32 [3, 2048, 2048], P(None, 'ep', 'tp')
- grad_b_qkv: float32 [3, 16, 128], P(None, 'tp', 'ep')
- grad_w_out: float32 [2048, 2048], P('tp', 'ep')
- grad_norm2_gain: float32 [2048], P('ep')
- grad_w_router: float32 [2048, 8], P('ep')
- grad_w_sgate: float32 [2048], P('ep')
- grad_w_shared_gu: float32 [2, 2048, 5632], P(None, 'ep', 'tp')
- grad_w_shared_down: float32 [5632, 2048], P('tp', 'ep')
- grad_w_expert_gu: float32 [8, 2, 2048, 1408], P('ep', None, None, 'tp')
- grad_w_expert_down: float32 [8, 1408, 2048], P('ep', 'tp')
Inputs may be any that keep to these rules, and one draw needn't show every extreme that they name: `routes`: each row names 4 different experts. Among the rows of one sequence no expert is named more than 400 times, and in every draw some expert is named exactly 400 times within some sequence.
All inputs are finite; a program needn't handle non-finite values.
Results may differ from a plain program's by a relative error of at most 0.024.
Values may be sent and summed in bfloat16 or wider, within the bound.
A program may use at most 384 MiB of HBM per device.

v0:
```python
import jax
import jax.numpy as jnp
from jax import lax
from jax.sharding import PartitionSpec as P

norm_eps = 1e-06
rope_base = 1000000.0
masked_score = -1e30


def contract(left_side, right_side, left_dim, right_dim):
    return lax.dot_general(
        left_side,
        right_side,
        (((left_dim,), (right_dim,)), ((), ())),
        preferred_element_type=jnp.float32,
    )


def rms_forward(hidden, gain_vector):
    inv_scale = lax.rsqrt(jnp.mean(hidden * hidden, axis=-1, keepdims=True) + norm_eps)
    normed = hidden * inv_scale
    return (normed * gain_vector, normed, inv_scale)


def rms_backward(grad_normed_out, gain_vector, normed, inv_scale):
    grad_scaled = grad_normed_out * gain_vector
    grad_gain = jnp.sum(grad_normed_out * normed, axis=0)
    inner_mean = jnp.mean(grad_scaled * normed, axis=-1, keepdims=True)
    return (inv_scale * (grad_scaled - normed * inner_mean), grad_gain)


def rope_tables(length, head_dim):
    half_dim = head_dim // 2
    frequency = rope_base ** (-(jnp.arange(half_dim, dtype=jnp.float32) * 2.0) / head_dim)
    angles = jnp.arange(length, dtype=jnp.float32)[:, None] * frequency[None, :]
    cosine_table = jnp.concatenate([jnp.cos(angles), jnp.cos(angles)], axis=-1)[:, None, :]
    sine_table = jnp.concatenate([jnp.sin(angles), jnp.sin(angles)], axis=-1)[:, None, :]
    return (cosine_table, sine_table)


def rotate_forward(values, cosine_table, sine_table):
    half_dim = values.shape[-1] // 2
    turned = jnp.concatenate([-values[..., half_dim:], values[..., :half_dim]], axis=-1)
    return values * cosine_table + turned * sine_table


def rotate_backward(grad_rows, cosine_table, sine_table):
    half_dim = grad_rows.shape[-1] // 2
    scaled = grad_rows * sine_table
    turned = jnp.concatenate([scaled[..., half_dim:], -scaled[..., :half_dim]], axis=-1)
    return grad_rows * cosine_table + turned


def gated_backward(grad_act, gate_up):
    sigmoid_gate = jax.nn.sigmoid(gate_up[0])
    grad_gate = grad_act * gate_up[1] * sigmoid_gate * (1.0 + gate_up[0] * (1.0 - sigmoid_gate))
    grad_up = grad_act * gate_up[0] * sigmoid_gate
    return jnp.stack([grad_gate, grad_up]).astype(jnp.bfloat16)


def slot_table(routes, experts, capacity):
    pair_experts = routes.reshape(-1)
    choose = (pair_experts[:, None] == jnp.arange(experts, dtype=jnp.int32)[None, :]).astype(
        jnp.int32
    )
    before = jnp.cumsum(choose, axis=0) - choose
    slot_number = jnp.sum(before * choose, axis=1)
    slot_dest = pair_experts * capacity + slot_number
    pair_count = pair_experts.shape[0]
    slot_owner = (
        jnp.full((experts * capacity,), pair_count, jnp.int32)
        .at[slot_dest]
        .set(jnp.arange(pair_count, dtype=jnp.int32))
    )
    return (slot_dest, slot_owner)


def per_device(
    tokens,
    norm1_gain,
    w_qkv,
    b_qkv,
    w_out,
    norm2_gain,
    w_router,
    w_sgate,
    w_shared_gu,
    w_shared_down,
    w_expert_gu,
    w_expert_down,
    routes,
    grad_out,
):
    seq_rows, features = tokens.shape
    top_count = routes.shape[1]
    expert_count = w_router.shape[1]
    heads_here = b_qkv.shape[1]
    head_dim = b_qkv.shape[2]
    lane_count = lax.axis_size("tp")
    lane_index = lax.axis_index("tp")
    capacity = lane_count * (5 * seq_rows * top_count // (4 * expert_count * lane_count))
    out_rows = seq_rows // lane_count
    row_start = lane_index * out_rows
    score_scale = head_dim ** (-0.5)
    residual = tokens.astype(jnp.float32)
    normed_one, unit_one, scale_one = rms_forward(residual, norm1_gain)
    low_one = normed_one.astype(jnp.bfloat16)
    qkv_pre = jnp.einsum("ld,cde->cle", low_one, w_qkv, preferred_element_type=jnp.float32)
    qkv_pre = qkv_pre + b_qkv.reshape(3, 1, -1).astype(jnp.float32)
    cosine_table, sine_table = rope_tables(seq_rows, head_dim)
    shaped = qkv_pre.reshape(3, seq_rows, heads_here, head_dim)
    queries = rotate_forward(shaped[0], cosine_table, sine_table).astype(jnp.bfloat16)
    key_rows = rotate_forward(shaped[1], cosine_table, sine_table).astype(jnp.bfloat16)
    value_rows = shaped[2].astype(jnp.bfloat16)
    positions = jnp.arange(seq_rows)
    causal = positions[None, :] <= positions[:, None]

    def attn_scores():
        raw_scores = (
            jnp.einsum("qhd,khd->hqk", queries, key_rows, preferred_element_type=jnp.float32)
            * score_scale
        )
        return jnp.where(causal[None], raw_scores, masked_score)

    scores = attn_scores()
    score_peak = jnp.max(scores, axis=-1, keepdims=True)
    log_total = score_peak + jnp.log(jnp.sum(jnp.exp(scores - score_peak), axis=-1, keepdims=True))
    attn_probs = jnp.exp(scores - log_total).astype(jnp.bfloat16)
    attn_mixed = jnp.einsum(
        "hqk,khd->qhd", attn_probs, value_rows, preferred_element_type=jnp.float32
    )
    attn_mixed = attn_mixed.reshape(seq_rows, -1).astype(jnp.bfloat16)
    attn_total = lax.psum(jnp.dot(attn_mixed, w_out, preferred_element_type=jnp.float32), "tp")
    hidden = residual + attn_total
    normed_two, unit_two, scale_two = rms_forward(hidden, norm2_gain)
    low_two = normed_two.astype(jnp.bfloat16)
    router_probs = jax.nn.softmax(
        jnp.dot(low_two, w_router, preferred_element_type=jnp.float32), axis=-1
    )
    route_hits = (
        routes[:, :, None] == jnp.arange(expert_count, dtype=jnp.int32)[None, None, :]
    ).astype(jnp.float32)
    gate_values = jnp.sum(router_probs[:, None, :] * route_hits, axis=-1)
    shared_gate = jax.nn.sigmoid(jnp.dot(low_two, w_sgate, preferred_element_type=jnp.float32))
    shared_gu = jnp.einsum("ld,cdf->clf", low_two, w_shared_gu, preferred_element_type=jnp.float32)
    shared_act = (jax.nn.silu(shared_gu[0]) * shared_gu[1]).astype(jnp.bfloat16)
    shared_part = jnp.dot(shared_act, w_shared_down, preferred_element_type=jnp.float32)
    slot_dest, slot_owner = slot_table(routes, expert_count, capacity)
    slot_source = (slot_owner // top_count).reshape(expert_count, capacity)
    owner_table = slot_owner.reshape(expert_count, capacity)
    padded_two = jnp.concatenate([low_two, jnp.zeros((1, features), jnp.bfloat16)], axis=0)
    arrived = lax.all_to_all(padded_two[slot_source], "ep", split_axis=0, concat_axis=0, tiled=True)
    expert_in = arrived.reshape(-1, features)
    gate_up_weight = w_expert_gu[0]
    down_weight = w_expert_down[0]
    gate_up = jnp.einsum(
        "rd,cdf->crf", expert_in, gate_up_weight, preferred_element_type=jnp.float32
    )
    expert_act = (jax.nn.silu(gate_up[0]) * gate_up[1]).astype(jnp.bfloat16)
    expert_part = jnp.dot(expert_act, down_weight, preferred_element_type=jnp.float32).astype(
        jnp.bfloat16
    )
    expert_part = expert_part.reshape(expert_count, capacity, features)
    returned = lax.all_to_all(expert_part, "ep", split_axis=0, concat_axis=0, tiled=True)
    return_table = returned.reshape(-1, features)
    return_table = jnp.concatenate(
        [return_table, jnp.zeros((1, features), return_table.dtype)], axis=0
    )
    picked = return_table[slot_dest].reshape(seq_rows, top_count, features)
    expert_sum = jnp.zeros((seq_rows, features), jnp.float32)
    for route_slot in range(top_count):
        expert_sum = expert_sum + gate_values[:, route_slot, None] * picked[:, route_slot].astype(
            jnp.float32
        )
    mlp_total = lax.psum(
        (shared_gate[:, None] * shared_part + expert_sum).astype(jnp.bfloat16), "tp"
    ).astype(jnp.float32)
    output = hidden + mlp_total
    output_rows = lax.dynamic_slice_in_dim(output, row_start, out_rows, 0).astype(jnp.bfloat16)
    grad_output = grad_out.astype(jnp.float32)
    grad_sout = (shared_gate[:, None] * grad_output).astype(jnp.bfloat16)
    grad_shared_down = contract(shared_act, grad_sout, 0, 0)
    grad_sgu = gated_backward(contract(grad_sout, w_shared_down, 1, 1), shared_gu)
    grad_shared_gu = jnp.einsum(
        "ld,clf->cdf", low_two, grad_sgu, preferred_element_type=jnp.float32
    )
    grad_low_two = jnp.einsum(
        "clf,cdf->ld", grad_sgu, w_shared_gu, preferred_element_type=jnp.float32
    )
    shared_dot = jnp.sum(grad_output * shared_part, axis=-1)
    gate_dot = jnp.sum(grad_output[:, None, :] * picked.astype(jnp.float32), axis=-1)
    gate_flat = jnp.concatenate([gate_values.reshape(-1), jnp.zeros((1,), jnp.float32)])
    padded_grad = jnp.concatenate([grad_output, jnp.zeros((1, features), jnp.float32)], axis=0)
    sent_grads = (padded_grad[slot_source] * gate_flat[owner_table][:, :, None]).astype(
        jnp.bfloat16
    )
    grad_arrived = lax.all_to_all(sent_grads, "ep", split_axis=0, concat_axis=0, tiled=True)
    grad_arrived = grad_arrived.reshape(-1, features)
    grad_expert_down = contract(expert_act, grad_arrived, 0, 0)
    grad_egu = gated_backward(contract(grad_arrived, down_weight, 1, 1), gate_up)
    grad_expert_gu = jnp.einsum(
        "rd,crf->cdf", expert_in, grad_egu, preferred_element_type=jnp.float32
    )
    grad_sent = jnp.einsum(
        "crf,cdf->rd", grad_egu, gate_up_weight, preferred_element_type=jnp.float32
    ).astype(jnp.bfloat16)
    grad_returned = lax.all_to_all(
        grad_sent.reshape(expert_count, capacity, features),
        "ep",
        split_axis=0,
        concat_axis=0,
        tiled=True,
    )
    grad_pairs = grad_returned.reshape(-1, features)[slot_dest].reshape(
        seq_rows, top_count, features
    )
    grad_low_two = grad_low_two + jnp.sum(grad_pairs.astype(jnp.float32), axis=1)
    grad_low_two, gate_dot, shared_dot = (
        lax.psum(grad_low_two.astype(jnp.bfloat16), "tp").astype(jnp.float32),
        lax.psum(gate_dot.astype(jnp.bfloat16), "tp").astype(jnp.float32),
        lax.psum(shared_dot.astype(jnp.bfloat16), "tp").astype(jnp.float32),
    )
    grad_sgate_logit = (shared_dot * shared_gate * (1.0 - shared_gate)).astype(jnp.bfloat16)
    grad_sgate = contract(low_two, grad_sgate_logit, 0, 0)
    grad_probs = jnp.sum(gate_dot[:, :, None] * route_hits, axis=1)
    grad_logits = router_probs * (
        grad_probs - jnp.sum(router_probs * grad_probs, axis=-1, keepdims=True)
    )
    grad_logits = grad_logits.astype(jnp.bfloat16)
    grad_router = contract(low_two, grad_logits, 0, 0)
    grad_low_two = (
        grad_low_two
        + grad_sgate_logit.astype(jnp.float32)[:, None] * w_sgate.astype(jnp.float32)[None, :]
    )
    grad_low_two = grad_low_two + contract(grad_logits, w_router, 1, 1)
    grad_hidden_norm, grad_norm_two = rms_backward(grad_low_two, norm2_gain, unit_two, scale_two)
    grad_hidden = grad_output + grad_hidden_norm
    grad_attn = grad_hidden.astype(jnp.bfloat16)
    grad_out_weight = contract(attn_mixed, grad_attn, 0, 0)
    grad_mixed = (
        contract(grad_attn, w_out, 1, 1)
        .astype(jnp.bfloat16)
        .reshape(seq_rows, heads_here, head_dim)
    )
    again_probs = jnp.exp(attn_scores() - log_total)
    grad_values = jnp.einsum(
        "hqk,qhd->khd",
        again_probs.astype(jnp.bfloat16),
        grad_mixed,
        preferred_element_type=jnp.float32,
    )
    grad_probs_attn = jnp.einsum(
        "qhd,khd->hqk", grad_mixed, value_rows, preferred_element_type=jnp.float32
    )
    grad_scores = again_probs * (
        grad_probs_attn - jnp.sum(again_probs * grad_probs_attn, axis=-1, keepdims=True)
    )
    grad_scores = grad_scores.astype(jnp.bfloat16)
    grad_queries = (
        jnp.einsum("hqk,khd->qhd", grad_scores, key_rows, preferred_element_type=jnp.float32)
        * score_scale
    )
    grad_keys = (
        jnp.einsum("hqk,qhd->khd", grad_scores, queries, preferred_element_type=jnp.float32)
        * score_scale
    )
    grad_pre = jnp.stack(
        [
            rotate_backward(grad_queries, cosine_table, sine_table),
            rotate_backward(grad_keys, cosine_table, sine_table),
            grad_values,
        ]
    )
    grad_pre = grad_pre.reshape(3, seq_rows, -1).astype(jnp.bfloat16)
    grad_bias = jnp.sum(grad_pre.astype(jnp.float32), axis=1).reshape(3, heads_here, head_dim)
    grad_qkv = jnp.einsum("ld,cle->cde", low_one, grad_pre, preferred_element_type=jnp.float32)
    grad_low_one = lax.psum(
        jnp.einsum("cle,cde->ld", grad_pre, w_qkv, preferred_element_type=jnp.float32).astype(
            jnp.bfloat16
        ),
        "tp",
    ).astype(jnp.float32)
    grad_input_norm, grad_norm_one = rms_backward(grad_low_one, norm1_gain, unit_one, scale_one)
    grad_tokens = lax.dynamic_slice_in_dim(grad_hidden + grad_input_norm, row_start, out_rows, 0)
    summed = (
        lax.psum_scatter(grad_norm_one, "ep", scatter_dimension=0, tiled=True),
        lax.psum_scatter(grad_qkv, "ep", scatter_dimension=1, tiled=True),
        lax.psum_scatter(grad_bias, "ep", scatter_dimension=2, tiled=True),
        lax.psum_scatter(grad_out_weight, "ep", scatter_dimension=1, tiled=True),
        lax.psum_scatter(grad_norm_two, "ep", scatter_dimension=0, tiled=True),
        lax.psum_scatter(grad_router, "ep", scatter_dimension=0, tiled=True),
        lax.psum_scatter(grad_sgate, "ep", scatter_dimension=0, tiled=True),
        lax.psum_scatter(grad_shared_gu, "ep", scatter_dimension=1, tiled=True),
        lax.psum_scatter(grad_shared_down, "ep", scatter_dimension=1, tiled=True),
    )
    return (
        output_rows,
        grad_tokens,
        summed[0],
        summed[1],
        summed[2],
        summed[3],
        summed[4],
        summed[5],
        summed[6],
        summed[7],
        summed[8],
        grad_expert_gu[None],
        grad_expert_down[None],
    )


def solution(mesh):
    return jax.shard_map(
        per_device,
        mesh=mesh,
        in_specs=(
            P("ep", None),
            P(),
            P(None, None, "tp"),
            P(None, "tp", None),
            P("tp", None),
            P(),
            P(),
            P(),
            P(None, None, "tp"),
            P("tp", None),
            P("ep", None, None, "tp"),
            P("ep", "tp", None),
            P("ep", None),
            P("ep", None),
        ),
        out_specs=(
            P(("ep", "tp"), None),
            P(("ep", "tp"), None),
            P("ep"),
            P(None, "ep", "tp"),
            P(None, "tp", "ep"),
            P("tp", "ep"),
            P("ep"),
            P("ep", None),
            P("ep"),
            P(None, "ep", "tp"),
            P("tp", "ep"),
            P("ep", None, None, "tp"),
            P("ep", "tp", None),
        ),
        check_vma=False,
    )
```

profile of v0, /device:TPU:0, one launch (start us, length us, event | category | flops | bytes accessed | tf_op | source)
XLA Modules:
  0.0 1859.8 jit_solution(4364813825440306006)
XLA Ops:
  37.6 21.9 %scatter_custom_fusion = s32[3200]{0:T(1024)S(1)} fusion(s32[2560]{0:T(1024)S(1)} %get-tuple-element.96, s32[2560]{0:T(1024)S(1)} %iota.45, s32[]{:T(128)} %constant.23.clone.1), kind=kCustom, calls=%fused_computation.175 | custom fusion | bytes 12804 | tf_op jit(solution)/shard_map/scatter | solution.py:74
  59.8 164.4 %all-reduce.13.cloned.1.call-done = f32[640,2048]{1,0:T(8,128)} async-done(((f32[640,2048]{1,0:T(8,128)}), f32[640,2048]{1,0:T(8,128)}) %all-reduce.13.cloned.1.call-update) | async-done | bytes 5242896 | tf_op jit(solution)/shard_map/psum | solution.py:134
  234.4 27.7 %gather_fusion = bf16[3200,2048]{1,0:T(8,128)(2,1)} fusion(bf16[641,2048]{1,0:T(8,128)(2,1)} %concatenate.36, s32[4096]{0:T(1024)S(1)} %pad_clamp_fusion.1), kind=kCustom, calls=%fused_computation | custom fusion | bytes 26227200 | tf_op jit(solution)/shard_map/gather | solution.py:153
  262.2 148.5 %all_to_all.20 = bf16[8,400,2048]{2,1,0:T(8,128)(2,1)S(1)} all-to-all(bf16[8,400,2048]{2,1,0:T(8,128)(2,1)} %bitcast.232), channel_id=1, replica_groups=mesh['ep'=8,'tp'=4] {'ep'}, dimensions={0} | all-to-all | bytes 26214400 | tf_op jit(solution)/shard_map/all_to_all | solution.py:153
  450.5 27.3 %gather_fusion.2 = f32[3200,2048]{1,0:T(8,128)} fusion(f32[641,2048]{1,0:T(8,128)} %concatenate.38, s32[4096]{0:T(1024)S(1)} %pad_clamp_fusion.1), kind=kCustom, calls=%fused_computation.2 | custom fusion | bytes 52441600 | tf_op jit(solution)/shard_map/gather | solution.py:195
  512.8 74.1 %all-to-all-done.1 = bf16[8,400,2048]{2,1,0:T(8,128)(2,1)} async-done(((bf16[8,400,2048]{2,1,0:T(8,128)(2,1)}), bf16[8,400,2048]{2,1,0:T(8,128)(2,1)}, u32[]{:S(2)}, u32[]{:S(2)}) %all-to-all-start.1) | async-done | bytes 13107232 | tf_op jit(solution)/shard_map/all_to_all | solution.py:165
  598.3 26.6 %gather_fusion.1 = bf16[2560,2048]{1,0:T(8,128)(2,1)} fusion(bf16[3201,2048]{1,0:T(8,128)(2,1)} %concatenate.37, s32[3072]{0:T(1024)S(1)} %pad_clamp_fusion.3), kind=kCustom, calls=%fused_computation.1 | custom fusion | bytes 20981760 | tf_op jit(solution)/shard_map/gather | solution.py:170
  689.8 147.5 %all_to_all.21 = bf16[8,400,2048]{2,1,0:T(8,128)(2,1)S(1)} all-to-all(bf16[8,400,2048]{2,1,0:T(8,128)(2,1)S(1)} %multiply_convert_fusion), channel_id=1, replica_groups=mesh['ep'=8,'tp'=4] {'ep'}, dimensions={0} | all-to-all | bytes 26214400 | tf_op jit(solution)/shard_map/all_to_all | solution.py:198
  837.3 17.0 fusion.27
  875.1 144.5 %all-to-all-done.3 = bf16[8,400,2048]{2,1,0:T(8,128)(2,1)} async-done(((bf16[8,400,2048]{2,1,0:T(8,128)(2,1)}), bf16[8,400,2048]{2,1,0:T(8,128)(2,1)}, u32[]{:S(2)}, u32[]{:S(2)}) %all-to-all-start.3) | async-done | bytes 13107232 | tf_op jit(solution)/shard_map/all_to_all | solution.py:208
  1019.6 26.8 %gather_fusion.4 = bf16[2560,2048]{1,0:T(8,128)(2,1)} fusion(bf16[3200,2048]{1,0:T(8,128)(2,1)} %bitcast.36, s32[3072]{0:T(1024)S(1)} %pad_clamp_fusion.2), kind=kCustom, calls=%fused_computation.4 | custom fusion | bytes 20981760 | tf_op jit(solution)/shard_map/gather | solution.py:215
  1046.4 19.0 %reshape.317 = f32[640,4,2048]{2,1,0:T(4,128)} reshape(bf16[2560,2048]{1,0:T(8,128)(2,1)} %gather_fusion.4) | data formatting | bytes 31457280 | tf_op jit(solution)/shard_map/convert_element_type | solution.py:218
  1065.4 18.5 reduce_sum.162
  1113.3 31.4 %fusion.69 = (bf16[640,1,2048]{2,1,0:T(2,128)(2,1)S(1)}, bf16[640,1,2048]{2,1,0:T(2,128)(2,1)S(1)}, bf16[640,1,2048]{2,1,0:T(2,128)(2,1)S(1)}, bf16[640,1,2048]{2,1,0:T(2,128)(2,1)S(1)}) fusion(bf16[640,4,2048]{2,1,0:T(4,128)(2,1)} %reshape.304), kind=kLoop, calls=%fused_computation.195 | loop fusion | bytes 20971520 | tf_op jit(solution)/shard_map/slice | solution.py:173
  1144.8 17.1 fusion.4
  1161.9 36.5 %all-reduce.15.cloned.1.call-done = bf16[640,2048]{1,0:T(8,128)(2,1)} async-done(((bf16[640,2048]{1,0:T(8,128)(2,1)}), bf16[640,2048]{1,0:T(8,128)(2,1)}) %all-reduce.15.cloned.1.call-update) | async-done | bytes 2621456 | tf_op jit(solution)/shard_map/psum | solution.py:220
  1314.9 32.4 %reduce-scatter.15.cloned.1.call-done = f32[2,256,1408]{1,2,0:T(8,128)} async-done(((f32[2,2048,1408]{1,2,0:T(8,128)}), f32[2,256,1408]{1,2,0:T(8,128)}) %reduce-scatter.15.cloned.1.call-update) | async-done | bytes 2883600 | tf_op jit(solution)/shard_map/reduce_scatter | solution.py:294
  1350.6 33.6 %reduce-scatter.19.cloned.1.call-done = f32[16,12]{1,0:T(8,128)} async-done(((f32[128,12]{1,0:T(8,128)}), f32[16,12]{1,0:T(8,128)}) %reduce-scatter.19.cloned.1.call-update) | async-done | bytes 784
  1385.7 189.8 %all-reduce.17.cloned.1.call-done = (bf16[640,2048]{1,0:T(8,128)(2,1)}, bf16[640,2048]{1,0:T(8,128)(2,1)}) async-done(((bf16[640,2048]{1,0:T(8,128)(2,1)}, bf16[640,2048]{1,0:T(8,128)(2,1)}), (bf16[640,2048]{1,0:T(8,128)(2,1)}, bf16[640,2048]{1,0:T(8,128)(2,1)})) %all-reduce.17.cloned.1.call-update) | async-done | bytes 5242896 | tf_op jit(solution)/shard_map/psum | solution.py:176
  1582.7 23.8 %all-reduce.6 = (f32[2048]{0:T(1024)S(1)}, f32[2048]{0:T(1024)S(1)}, f32[2048]{0:T(1024)S(1)}) all-reduce(f32[2048]{0:T(1024)S(1)} %get-tuple-element.93, f32[2048]{0:T(1024)S(1)} %copy-done.55, f32[2048]{0:T(1024)S(1)} %bitcast.256), channel_id=2, replica_groups=mesh['ep'=8,'tp'=4] {'ep'}, use_global_device_ids=true, to_apply=%region_26.27.clone | all-reduce | flops 6144 | bytes 49152
  1614.7 55.1 %reduce-scatter.9.cloned.1.call-done = f32[3,256,512]{1,2,0:T(8,128)} async-done(((f32[3,2048,512]{1,2,0:T(8,128)}), f32[3,256,512]{1,2,0:T(8,128)}) %reduce-scatter.9.cloned.1.call-update) | async-done | bytes 1572880 | tf_op jit(solution)/shard_map/reduce_scatter | solution.py:288
  1672.8 87.9 %reduce-scatter.17.cloned.1.call-done = f32[1408,256]{1,0:T(8,128)} async-done(((f32[1408,2048]{1,0:T(8,128)}), f32[1408,256]{1,0:T(8,128)}) %reduce-scatter.17.cloned.1.call-update) | async-done | bytes 1441808 | tf_op jit(solution)/shard_map/reduce_scatter | solution.py:295
  1760.7 37.1 %reduce-scatter.13.cloned.1.call-done = f32[256,8]{0,1:T(8,128)} async-done(((f32[2048,8]{0,1:T(8,128)}), f32[256,8]{0,1:T(8,128)}) %reduce-scatter.13.cloned.1.call-update) | async-done | bytes 8208 | tf_op jit(solution)/shard_map/reduce_scatter | solution.py:292
  1797.8 55.0 %reduce-scatter.11.cloned.1.call-done = f32[512,256]{1,0:T(8,128)} async-done(((f32[512,2048]{1,0:T(8,128)}), f32[512,256]{1,0:T(8,128)}) %reduce-scatter.11.cloned.1.call-update) | async-done | bytes 524304 | tf_op jit(solution)/shard_map/reduce_scatter | solution.py:290
  (303 shorter events, 380.0 us)
Async XLA Ops:
  7.2 403.5 %copy-start = (bf16[1,2,2048,352]{2,3,1,0:T(8,128)(2,1)S(1)}, bf16[1,2,2048,352]{2,3,1,0:T(8,128)(2,1)}, u32[]{:S(2)}) copy-start(bf16[1,2,2048,352]{2,3,1,0:T(8,128)(2,1)} %param.24) | copy-start | bytes 8650756
  7.2 217.0 %all-reduce.13.cloned.1.call-start = ((), (), s32[]{:S(2)}) async-start(), calls=%async_computation.10 | async-start | bytes 10485760 | tf_op jit(solution)/shard_map/psum | solution.py:134
  37.6 21.9 %copy-start.50 = (s32[2560]{0:T(1024)}, s32[2560]{0:T(1024)S(1)}, u32[]{:S(2)}) copy-start(s32[2560]{0:T(1024)S(1)} %get-tuple-element.96) | copy-start | bytes 30724
  59.8 170.8 %copy-start.44 = (f32[2048]{0:T(1024)S(1)}, f32[2048]{0:T(1024)}, u32[]{:S(2)}) copy-start(f32[2048]{0:T(1024)} %param.19) | copy-start | bytes 24580
  436.5 150.4 %all-to-all-start.1 = ((bf16[8,400,2048]{2,1,0:T(8,128)(2,1)}), bf16[8,400,2048]{2,1,0:T(8,128)(2,1)}, u32[]{:S(2)}, u32[]{:S(2)}) async-start(bf16[8,400,2048]{2,1,0:T(8,128)(2,1)} %bitcast.239), calls=%async_computation.1 | async-start | bytes 26214400 | tf_op jit(solution)/shard_map/all_to_all | solution.py:165
  450.5 27.3 %copy-start.52 = (s32[2560]{0:T(1024)S(1)}, s32[2560]{0:T(1024)}, u32[]{:S(2)}) copy-start(s32[2560]{0:T(1024)} %get-tuple-element.95) | copy-start | bytes 30724
  450.5 27.3 %copy-start.34 = (bf16[2048,8]{0,1:T(8,128)(2,1)S(1)}, bf16[2048,8]{0,1:T(8,128)(2,1)}, u32[]{:S(2)}) copy-start(bf16[2048,8]{0,1:T(8,128)(2,1)} %param.20) | copy-start | bytes 98308
  689.7 147.5 %copy-start.65 = (bf16[1,352,2048]{2,1,0:T(8,128)(2,1)S(1)}, bf16[1,352,2048]{2,1,0:T(8,128)(2,1)}, u32[]{:S(2)}) copy-start(bf16[1,352,2048]{2,1,0:T(8,128)(2,1)} %param.25) | copy-start | bytes 4325380
  869.5 150.2 %all-to-all-start.3 = ((bf16[8,400,2048]{2,1,0:T(8,128)(2,1)}), bf16[8,400,2048]{2,1,0:T(8,128)(2,1)}, u32[]{:S(2)}, u32[]{:S(2)}) async-start(bf16[8,400,2048]{2,1,0:T(8,128)(2,1)} %bitcast.240), calls=%async_computation.3 | async-start | bytes 26214400 | tf_op jit(solution)/shard_map/all_to_all | solution.py:208
  875.0 323.4 %all-reduce.15.cloned.1.call-start = ((), (), s32[]{:S(2)}) async-start(), calls=%async_computation.11 | async-start | bytes 5242880 | tf_op jit(solution)/shard_map/psum | solution.py:220
  1097.5 249.8 %reduce-scatter.15.cloned.1.call-start = ((), (), s32[]{:S(2)}) async-start(), calls=%async_computation.15 | async-start | bytes 25952256 | tf_op jit(solution)/shard_map/reduce_scatter | solution.py:294
  1111.9 272.3 %reduce-scatter.19.cloned.1.call-start = ((), (), s32[]{:S(2)}) async-start(), calls=%async_computation.17 | async-start | bytes 73728
  1113.3 31.5 %copy-start.59 = (f32[640]{0:T(1024)S(1)}, f32[640]{0:T(1024)}, u32[]{:S(2)}) copy-start(f32[640]{0:T(1024)} %copy-done.58) | copy-start | bytes 7684
  1144.8 53.7 %copy-start.35 = (bf16[2048,8]{0,1:T(8,128)(2,1)S(1)}, bf16[2048,8]{0,1:T(8,128)(2,1)}, u32[]{:S(2)}) copy-start(bf16[2048,8]{0,1:T(8,128)(2,1)} %param.20) | copy-start | bytes 98308
  1144.8 53.7 %copy-start.45 = (f32[2048]{0:T(1024)S(1)}, f32[2048]{0:T(1024)}, u32[]{:S(2)}) copy-start(f32[2048]{0:T(1024)} %param.19) | copy-start | bytes 24580
  1144.8 53.6 %copy-start.49 = (f32[640]{0:T(1024)S(1)}, f32[640]{0:T(1024)}, u32[]{:S(2)}) copy-start(f32[640]{0:T(1024)} %copy-done.48) | copy-start | bytes 7684
  1198.5 21.3 %slice-start = ((s8[6553600]{0:T(1024)(128)(4,1)}), s8[4194304]{0:T(1024)(128)(4,1)S(1)}, s32[]{:S(2)}) async-start(s8[6553600]{0:T(1024)(128)(4,1)} %bitcast.229), calls=%async_computation.19 | async-start | bytes 8388608
  1249.8 325.7 %all-reduce.17.cloned.1.call-start = ((), (), s32[]{:S(2)}) async-start(), calls=%async_computation.18 | async-start | bytes 10485760 | tf_op jit(solution)/shard_map/psum | solution.py:176
  1258.9 410.9 %reduce-scatter.9.cloned.1.call-start = ((), (), s32[]{:S(2)}) async-start(), calls=%async_computation.12 | async-start | bytes 14155776 | tf_op jit(solution)/shard_map/reduce_scatter | solution.py:288
  1269.9 490.8 %reduce-scatter.17.cloned.1.call-start = ((), (), s32[]{:S(2)}) async-start(), calls=%async_computation.16 | async-start | bytes 12976128 | tf_op jit(solution)/shard_map/reduce_scatter | solution.py:295
  1281.4 516.4 %reduce-scatter.13.cloned.1.call-start = ((), (), s32[]{:S(2)}) async-start(), calls=%async_computation.14 | async-start | bytes 73728 | tf_op jit(solution)/shard_map/reduce_scatter | solution.py:292
  1282.6 570.3 %reduce-scatter.11.cloned.1.call-start = ((), (), s32[]{:S(2)}) async-start(), calls=%async_computation.13 | async-start | bytes 4718592 | tf_op jit(solution)/shard_map/reduce_scatter | solution.py:290
  1314.9 260.6 %copy-start.8 = (bf16[640,2048]{1,0:T(8,128)(2,1)S(1)}, bf16[640,2048]{1,0:T(8,128)(2,1)}, u32[]{:S(2)}) copy-start(bf16[640,2048]{1,0:T(8,128)(2,1)} %param.14) | copy-start | bytes 7864324
  1608.5 244.3 %copy-start.1 = (bf16[1,2,2048,352]{2,3,1,0:T(8,128)(2,1)S(1)}, bf16[1,2,2048,352]{2,3,1,0:T(8,128)(2,1)}, u32[]{:S(2)}) copy-start(bf16[1,2,2048,352]{2,3,1,0:T(8,128)(2,1)} %param.24) | copy-start | bytes 8650756
  (65 other events, 408.3 us)
Sparse Core Ops, SparseCore 0:
  32.5 191.6 all-reduce.12
  1097.6 100.8 all-reduce.14
  1202.1 145.0 reduce-scatter.14
  1350.7 33.5 reduce-scatter.18
  1386.5 188.9 all-reduce.16
  1578.8 90.8 reduce-scatter.8
  1673.8 86.8 reduce-scatter.16
  1764.2 33.5 reduce-scatter.12
  1801.8 51.0 reduce-scatter.10
where the time goes:
time: 1870 us; the launch traced here: 1860 us
  waiting for transfers between devices  911 us (49%)
  blocking collectives  330 us (18%)
  local copies, waits for them, and re-layouts  266 us (14%)
  matrix products  219 us (12%)
  other arithmetic  107 us (6%)
    psum x1, waiting for transfers between devices, per_device(): lax.psum((shared_gate[:, None] * shared_part + expert_sum).astype(jnp.bfl...  190 us
    psum x1, waiting for transfers between devices, per_device(): lax.psum(jnp.dot(attn_mixed, w_out, preferred_element_type=jnp.float32),...  164 us
    all_to_all x1, blocking collectives, per_device(): lax.all_to_all(padded_two[slot_source], 'ep', split_axis=0, concat_axis=0...  149 us
    all_to_all x1, blocking collectives, per_device(): lax.all_to_all(sent_grads, 'ep', split_axis=0, concat_axis=0, tiled=True)  148 us
    all_to_all x1, waiting for transfers between devices, per_device(): lax.all_to_all(grad_sent.reshape(expert_count, capacity, features), 'ep',...  145 us
    reduce_scatter x1, waiting for transfers between devices, per_device(): lax.psum_scatter(grad_shared_down, 'ep', scatter_dimension=1, tiled=True)  87.9 us
    all_to_all x1, waiting for transfers between devices, per_device(): lax.all_to_all(expert_part, 'ep', split_axis=0, concat_axis=0, tiled=True)  74.1 us
    dot_general x9, matrix products, contract(): lax.dot_general(left_side, right_side, (((left_dim,), (right_dim,)), ((),...  70 us
  transfers between devices with their start and end apart: 11, of which 11 were waited for; matrix products, arithmetic and copies ran while one was open for 16% of the time, Pallas kernels for 0%

commit v1 on v0

--- a/solution.py
+++ b/solution.py
@@ -173,8 +173,11 @@
         expert_sum = expert_sum + gate_values[:, route_slot, None] * picked[:, route_slot].astype(
             jnp.float32
         )
-    mlp_total = lax.psum(
-        (shared_gate[:, None] * shared_part + expert_sum).astype(jnp.bfloat16), "tp"
+    mlp_total = jnp.sum(
+        lax.all_gather(
+            (shared_gate[:, None] * shared_part + expert_sum).astype(jnp.bfloat16), "tp"
+        ),
+        axis=0,
     ).astype(jnp.float32)
     output = hidden + mlp_total
     output_rows = lax.dynamic_slice_in_dim(output, row_start, out_rows, 0).astype(jnp.bfloat16)

time: 1870 us -> 1970 us (1.053)
  waiting for transfers between devices: 911 us -> 1000 us
    all_gather x0 -> x1, waiting for transfers between devices: none -> 182 us  [per_device(): lax.all_gather((shared_gate[:, None] * shared_part + expert_sum).astype(j...]
    psum x1, waiting for transfers between devices: 190 us -> 105 us  [per_device(): lax.psum(jnp.einsum('cle,cde->ld', grad_pre, w_qkv, preferred_element_typ...]
  transfers between devices with their start and end apart: 11 -> 12, of which waited for: 11 -> 12; matrix products, arithmetic and copies ran while one was open for 16% -> 15% of each run, Pallas kernels for 0% -> 0%
where the time goes in v1:
time: 1970 us; the launch traced here: 1960 us
  waiting for transfers between devices  1000 us (51%)
  blocking collectives  330 us (17%)
  local copies, waits for them, and re-layouts  265 us (13%)
  matrix products  219 us (11%)
  other arithmetic  115 us (6%)
    all_gather x1, waiting for transfers between devices, per_device(): lax.all_gather((shared_gate[:, None] * shared_part + expert_sum).astype(j...  182 us
    psum x1, waiting for transfers between devices, per_device(): lax.psum(jnp.dot(attn_mixed, w_out, preferred_element_type=jnp.float32),...  164 us
    all_to_all x1, blocking collectives, per_device(): lax.all_to_all(padded_two[slot_source], 'ep', split_axis=0, concat_axis=0...  149 us
    all_to_all x1, blocking collectives, per_device(): lax.all_to_all(sent_grads, 'ep', split_axis=0, concat_axis=0, tiled=True)  148 us
    all_to_all x1, waiting for transfers between devices, per_device(): lax.all_to_all(grad_sent.reshape(expert_count, capacity, features), 'ep',...  145 us
    psum x1, waiting for transfers between devices, per_device(): lax.psum(jnp.einsum('cle,cde->ld', grad_pre, w_qkv, preferred_element_typ...  105 us
    reduce_scatter x1, waiting for transfers between devices, per_device(): lax.psum_scatter(grad_shared_down, 'ep', scatter_dimension=1, tiled=True)  87.9 us
    all_to_all x1, waiting for transfers between devices, per_device(): lax.all_to_all(expert_part, 'ep', split_axis=0, concat_axis=0, tiled=True)  74.1 us
  transfers between devices with their start and end apart: 12, of which 12 were waited for; matrix products, arithmetic and copies ran while one was open for 15% of the time, Pallas kernels for 0%

profile of v1, /device:TPU:0, one launch (start us, length us, event | category | flops | bytes accessed | tf_op | source)
XLA Modules:
  0.0 1958.6 jit_solution(5527026491489622555)
XLA Ops:
  37.6 21.9 %scatter_custom_fusion = s32[3200]{0:T(1024)S(1)} fusion(s32[2560]{0:T(1024)S(1)} %get-tuple-element.96, s32[2560]{0:T(1024)S(1)} %iota.45, s32[]{:T(128)} %constant.24.clone.1), kind=kCustom, calls=%fused_computation.175 | custom fusion | bytes 12804 | tf_op jit(solution)/shard_map/scatter | solution.py:74
  59.8 164.4 %all-reduce.12.cloned.1.call-done = f32[640,2048]{1,0:T(8,128)} async-done(((f32[640,2048]{1,0:T(8,128)}), f32[640,2048]{1,0:T(8,128)}) %all-reduce.12.cloned.1.call-update) | async-done | bytes 5242896 | tf_op jit(solution)/shard_map/psum | solution.py:134
  234.5 27.7 %gather_fusion = bf16[3200,2048]{1,0:T(8,128)(2,1)} fusion(bf16[641,2048]{1,0:T(8,128)(2,1)} %concatenate.36, s32[4096]{0:T(1024)S(1)} %pad_clamp_fusion.1), kind=kCustom, calls=%fused_computation | custom fusion | bytes 26227200 | tf_op jit(solution)/shard_map/gather | solution.py:153
  262.2 148.5 %all_to_all.20 = bf16[8,400,2048]{2,1,0:T(8,128)(2,1)S(1)} all-to-all(bf16[8,400,2048]{2,1,0:T(8,128)(2,1)} %bitcast.233), channel_id=1, replica_groups=mesh['ep'=8,'tp'=4] {'ep'}, dimensions={0} | all-to-all | bytes 26214400 | tf_op jit(solution)/shard_map/all_to_all | solution.py:153
  450.5 27.3 %gather_fusion.2 = f32[3200,2048]{1,0:T(8,128)} fusion(f32[641,2048]{1,0:T(8,128)} %concatenate.38, s32[4096]{0:T(1024)S(1)} %pad_clamp_fusion.1), kind=kCustom, calls=%fused_computation.2 | custom fusion | bytes 52441600 | tf_op jit(solution)/shard_map/gather | solution.py:198
  512.8 74.1 %all-to-all-done.1 = bf16[8,400,2048]{2,1,0:T(8,128)(2,1)} async-done(((bf16[8,400,2048]{2,1,0:T(8,128)(2,1)}), bf16[8,400,2048]{2,1,0:T(8,128)(2,1)}, u32[]{:S(2)}, u32[]{:S(2)}) %all-to-all-start.1) | async-done | bytes 13107232 | tf_op jit(solution)/shard_map/all_to_all | solution.py:165
  598.3 26.6 %gather_fusion.1 = bf16[2560,2048]{1,0:T(8,128)(2,1)} fusion(bf16[3201,2048]{1,0:T(8,128)(2,1)} %concatenate.37, s32[3072]{0:T(1024)S(1)} %pad_clamp_fusion.3), kind=kCustom, calls=%fused_computation.1 | custom fusion | bytes 20981760 | tf_op jit(solution)/shard_map/gather | solution.py:170
  663.2 16.9 gather_fusion.3
  689.8 147.5 %all_to_all.21 = bf16[8,400,2048]{2,1,0:T(8,128)(2,1)S(1)} all-to-all(bf16[8,400,2048]{2,1,0:T(8,128)(2,1)S(1)} %multiply_convert_fusion), channel_id=1, replica_groups=mesh['ep'=8,'tp'=4] {'ep'}, dimensions={0} | all-to-all | bytes 26214400 | tf_op jit(solution)/shard_map/all_to_all | solution.py:201
  875.1 144.5 %all-to-all-done.3 = bf16[8,400,2048]{2,1,0:T(8,128)(2,1)} async-done(((bf16[8,400,2048]{2,1,0:T(8,128)(2,1)}), bf16[8,400,2048]{2,1,0:T(8,128)(2,1)}, u32[]{:S(2)}, u32[]{:S(2)}) %all-to-all-start.3) | async-done | bytes 13107232 | tf_op jit(solution)/shard_map/all_to_all | solution.py:211
  1019.6 26.8 %gather_fusion.4 = bf16[2560,2048]{1,0:T(8,128)(2,1)} fusion(bf16[3200,2048]{1,0:T(8,128)(2,1)} %bitcast.37, s32[3072]{0:T(1024)S(1)} %pad_clamp_fusion.2), kind=kCustom, calls=%fused_computation.4 | custom fusion | bytes 20981760 | tf_op jit(solution)/shard_map/gather | solution.py:218
  1046.4 19.0 reshape.317
  1065.4 18.5 reduce_sum.175
  1112.7 31.4 %fusion.69 = (bf16[640,1,2048]{2,1,0:T(2,128)(2,1)S(1)}, bf16[640,1,2048]{2,1,0:T(2,128)(2,1)S(1)}, bf16[640,1,2048]{2,1,0:T(2,128)(2,1)S(1)}, bf16[640,1,2048]{2,1,0:T(2,128)(2,1)S(1)}) fusion(bf16[640,4,2048]{2,1,0:T(4,128)(2,1)} %reshape.304), kind=kLoop, calls=%fused_computation.195 | loop fusion | bytes 20971520 | tf_op jit(solution)/shard_map/slice | solution.py:173
  1162.1 36.3 %all-reduce.14.cloned.1.call-done = bf16[640,2048]{1,0:T(8,128)(2,1)} async-done(((bf16[640,2048]{1,0:T(8,128)(2,1)}), bf16[640,2048]{1,0:T(8,128)(2,1)}) %all-reduce.14.cloned.1.call-update) | async-done | bytes 2621456 | tf_op jit(solution)/shard_map/psum | solution.py:223
  1314.3 32.9 %reduce-scatter.15.cloned.1.call-done = f32[2,256,1408]{1,2,0:T(8,128)} async-done(((f32[2,2048,1408]{1,2,0:T(8,128)}), f32[2,256,1408]{1,2,0:T(8,128)}) %reduce-scatter.15.cloned.1.call-update) | async-done | bytes 2883600 | tf_op jit(solution)/shard_map/reduce_scatter | solution.py:297
  1350.6 182.0 %all-gather.3.cloned.1.call-done = bf16[2560,2048]{1,0:T(8,128)(2,1)} async-done(((bf16[640,2048]{1,0:T(8,128)(2,1)}), bf16[2560,2048]{1,0:T(8,128)(2,1)}) %all-gather.3.cloned.1.call-update) | async-done | bytes 10485776 | tf_op jit(solution)/shard_map/all_gather | solution.py:177
  1542.2 25.5 %reduce-scatter.19.cloned.1.call-done = f32[16,12]{1,0:T(8,128)} async-done(((f32[128,12]{1,0:T(8,128)}), f32[16,12]{1,0:T(8,128)}) %reduce-scatter.19.cloned.1.call-update) | async-done | bytes 784
  1569.2 104.9 %all-reduce.16.cloned.1.call-done = bf16[640,2048]{1,0:T(8,128)(2,1)} async-done(((bf16[640,2048]{1,0:T(8,128)(2,1)}), bf16[640,2048]{1,0:T(8,128)(2,1)}) %all-reduce.16.cloned.1.call-update) | async-done | bytes 2621456 | tf_op jit(solution)/shard_map/psum | solution.py:281
  1682.4 23.8 %all-reduce.6 = (f32[2048]{0:T(1024)S(1)}, f32[2048]{0:T(1024)S(1)}, f32[2048]{0:T(1024)S(1)}) all-reduce(f32[2048]{0:T(1024)S(1)} %get-tuple-element.93, f32[2048]{0:T(1024)S(1)} %copy-done.54, f32[2048]{0:T(1024)S(1)} %bitcast.258), channel_id=3, replica_groups=mesh['ep'=8,'tp'=4] {'ep'}, use_global_device_ids=true, to_apply=%region_26.27.clone | all-reduce | flops 6144 | bytes 49152
  1711.7 56.9 %reduce-scatter.9.cloned.1.call-done = f32[3,256,512]{1,2,0:T(8,128)} async-done(((f32[3,2048,512]{1,2,0:T(8,128)}), f32[3,256,512]{1,2,0:T(8,128)}) %reduce-scatter.9.cloned.1.call-update) | async-done | bytes 1572880 | tf_op jit(solution)/shard_map/reduce_scatter | solution.py:291
  1771.6 87.9 %reduce-scatter.17.cloned.1.call-done = f32[1408,256]{1,0:T(8,128)} async-done(((f32[1408,2048]{1,0:T(8,128)}), f32[1408,256]{1,0:T(8,128)}) %reduce-scatter.17.cloned.1.call-update) | async-done | bytes 1441808 | tf_op jit(solution)/shard_map/reduce_scatter | solution.py:298
  1859.5 37.1 %reduce-scatter.13.cloned.1.call-done = f32[256,8]{0,1:T(8,128)} async-done(((f32[2048,8]{0,1:T(8,128)}), f32[256,8]{0,1:T(8,128)}) %reduce-scatter.13.cloned.1.call-update) | async-done | bytes 8208 | tf_op jit(solution)/shard_map/reduce_scatter | solution.py:295
  1896.6 54.9 %reduce-scatter.11.cloned.1.call-done = f32[512,256]{1,0:T(8,128)} async-done(((f32[512,2048]{1,0:T(8,128)}), f32[512,256]{1,0:T(8,128)}) %reduce-scatter.11.cloned.1.call-update) | async-done | bytes 524304 | tf_op jit(solution)/shard_map/reduce_scatter | solution.py:293
  (309 shorter events, 404.7 us)
Async XLA Ops:
  7.2 403.6 %copy-start = (bf16[1,2,2048,352]{2,3,1,0:T(8,128)(2,1)S(1)}, bf16[1,2,2048,352]{2,3,1,0:T(8,128)(2,1)}, u32[]{:S(2)}) copy-start(bf16[1,2,2048,352]{2,3,1,0:T(8,128)(2,1)} %param.24) | copy-start | bytes 8650756
  7.2 216.9 %all-reduce.12.cloned.1.call-start = ((), (), s32[]{:S(2)}) async-start(), calls=%async_computation.10 | async-start | bytes 10485760 | tf_op jit(solution)/shard_map/psum | solution.py:134
  59.8 170.9 %copy-start.43 = (f32[2048]{0:T(1024)S(1)}, f32[2048]{0:T(1024)}, u32[]{:S(2)}) copy-start(f32[2048]{0:T(1024)} %param.19) | copy-start | bytes 24580
  436.5 150.4 %all-to-all-start.1 = ((bf16[8,400,2048]{2,1,0:T(8,128)(2,1)}), bf16[8,400,2048]{2,1,0:T(8,128)(2,1)}, u32[]{:S(2)}, u32[]{:S(2)}) async-start(bf16[8,400,2048]{2,1,0:T(8,128)(2,1)} %bitcast.240), calls=%async_computation.1 | async-start | bytes 26214400 | tf_op jit(solution)/shard_map/all_to_all | solution.py:165
  450.5 27.3 %copy-start.51 = (s32[2560]{0:T(1024)S(1)}, s32[2560]{0:T(1024)}, u32[]{:S(2)}) copy-start(s32[2560]{0:T(1024)} %get-tuple-element.95) | copy-start | bytes 30724
  450.5 27.3 %copy-start.33 = (bf16[2048,8]{0,1:T(8,128)(2,1)S(1)}, bf16[2048,8]{0,1:T(8,128)(2,1)}, u32[]{:S(2)}) copy-start(bf16[2048,8]{0,1:T(8,128)(2,1)} %param.20) | copy-start | bytes 98308
  689.8 147.5 %copy-start.66 = (bf16[1,352,2048]{2,1,0:T(8,128)(2,1)S(1)}, bf16[1,352,2048]{2,1,0:T(8,128)(2,1)}, u32[]{:S(2)}) copy-start(bf16[1,352,2048]{2,1,0:T(8,128)(2,1)} %param.25) | copy-start | bytes 4325380
  869.4 150.1 %all-to-all-start.3 = ((bf16[8,400,2048]{2,1,0:T(8,128)(2,1)}), bf16[8,400,2048]{2,1,0:T(8,128)(2,1)}, u32[]{:S(2)}, u32[]{:S(2)}) async-start(bf16[8,400,2048]{2,1,0:T(8,128)(2,1)} %bitcast.241), calls=%async_computation.3 | async-start | bytes 26214400 | tf_op jit(solution)/shard_map/all_to_all | solution.py:211
  875.0 323.5 %all-reduce.14.cloned.1.call-start = ((), (), s32[]{:S(2)}) async-start(), calls=%async_computation.11 | async-start | bytes 5242880 | tf_op jit(solution)/shard_map/psum | solution.py:223
  1097.4 249.8 %reduce-scatter.15.cloned.1.call-start = ((), (), s32[]{:S(2)}) async-start(), calls=%async_computation.16 | async-start | bytes 25952256 | tf_op jit(solution)/shard_map/reduce_scatter | solution.py:297
  1111.9 420.6 %all-gather.3.cloned.1.call-start = ((), (), s32[]{:S(2)}) async-start(), calls=%async_computation.18 | async-start | bytes 13107200 | tf_op jit(solution)/shard_map/all_gather | solution.py:177
  1112.7 31.5 %copy-start.58 = (f32[640]{0:T(1024)S(1)}, f32[640]{0:T(1024)}, u32[]{:S(2)}) copy-start(f32[640]{0:T(1024)} %copy-done.57) | copy-start | bytes 7684
  1144.2 54.2 %copy-start.34 = (bf16[2048,8]{0,1:T(8,128)(2,1)S(1)}, bf16[2048,8]{0,1:T(8,128)(2,1)}, u32[]{:S(2)}) copy-start(bf16[2048,8]{0,1:T(8,128)(2,1)} %param.20) | copy-start | bytes 98308
  1144.2 54.2 %copy-start.44 = (f32[2048]{0:T(1024)S(1)}, f32[2048]{0:T(1024)}, u32[]{:S(2)}) copy-start(f32[2048]{0:T(1024)} %param.19) | copy-start | bytes 24580
  1144.2 54.2 %copy-start.48 = (f32[640]{0:T(1024)S(1)}, f32[640]{0:T(1024)}, u32[]{:S(2)}) copy-start(f32[640]{0:T(1024)} %copy-done.47) | copy-start | bytes 7684
  1161.2 406.5 %reduce-scatter.19.cloned.1.call-start = ((), (), s32[]{:S(2)}) async-start(), calls=%async_computation.19 | async-start | bytes 73728
  1249.8 424.3 %all-reduce.16.cloned.1.call-start = ((), (), s32[]{:S(2)}) async-start(), calls=%async_computation.12 | async-start | bytes 5242880 | tf_op jit(solution)/shard_map/psum | solution.py:281
  1258.8 509.8 %reduce-scatter.9.cloned.1.call-start = ((), (), s32[]{:S(2)}) async-start(), calls=%async_computation.13 | async-start | bytes 14155776 | tf_op jit(solution)/shard_map/reduce_scatter | solution.py:291
  1269.1 590.4 %reduce-scatter.17.cloned.1.call-start = ((), (), s32[]{:S(2)}) async-start(), calls=%async_computation.17 | async-start | bytes 12976128 | tf_op jit(solution)/shard_map/reduce_scatter | solution.py:298
  1281.2 615.5 %reduce-scatter.13.cloned.1.call-start = ((), (), s32[]{:S(2)}) async-start(), calls=%async_computation.15 | async-start | bytes 73728 | tf_op jit(solution)/shard_map/reduce_scatter | solution.py:295
  1282.4 669.2 %reduce-scatter.11.cloned.1.call-start = ((), (), s32[]{:S(2)}) async-start(), calls=%async_computation.14 | async-start | bytes 4718592 | tf_op jit(solution)/shard_map/reduce_scatter | solution.py:293
  1532.5 141.5 %copy-start.63 = (f32[2048]{0:T(1024)S(1)}, f32[2048]{0:T(1024)}, u32[]{:S(2)}) copy-start(f32[2048]{0:T(1024)} %param.15) | copy-start | bytes 24580
  1569.2 113.2 %copy-start.54 = (f32[2048]{0:T(1024)S(1)}, f32[2048]{0:T(1024)}, u32[]{:S(2)}) copy-start(f32[2048]{0:T(1024)} %get-tuple-element.91) | copy-start | bytes 24580
  1674.1 277.5 %copy-start.1 = (bf16[1,2,2048,352]{2,3,1,0:T(8,128)(2,1)S(1)}, bf16[1,2,2048,352]{2,3,1,0:T(8,128)(2,1)}, u32[]{:S(2)}) copy-start(bf16[1,2,2048,352]{2,3,1,0:T(8,128)(2,1)} %param.24) | copy-start | bytes 8650756
  (67 other events, 577.2 us)
Sparse Core Ops, SparseCore 0:
  32.5 191.6 all-reduce.11
  1097.5 100.8 all-reduce.13
  1202.1 145.0 reduce-scatter.14
  1348.6 183.8 all-gather.2
  1536.0 31.6 reduce-scatter.18
  1569.9 104.0 all-reduce.15
  1677.6 90.9 reduce-scatter.8
  1772.6 86.8 reduce-scatter.16
  1863.1 33.5 reduce-scatter.12
  1900.4 51.0 reduce-scatter.10
